TPU v7x, 32 devices: a whole 2x2x4 slice. The times are simulated.
32 devices in a mesh: grp: 2 (over y), col: 4 (over z), blk: 4 (over x, core).
Axes of the slice: x: 2, y: 2, z: 4, core: 2. Of those that a mesh axis runs over, the one named last changes fastest.
Arguments:
- boundary: bfloat16 [32, 192, 576], P(('grp', 'col'), 'blk'), parts along dimension 0, may hold values from -6 to 6
- row_tensor: bfloat16 [32, 6, 6, 6, 6], P(('grp', 'col')), parts along dimension 0, may hold values from -1.5 to 1.5
- left_proj: bfloat16 [32, 192, 576], P(('grp', 'col'), 'blk'), parts along dimension 0, may hold values from -0.75 to 0.75
- right_proj: bfloat16 [32, 192, 576], P(('grp', 'col'), 'blk'), parts along dimension 0, may hold values from -0.3125 to 0.3125
- leg_parity: int32 [32, 3, 6], P('grp'), parts along dimension 0, may hold values from 0 to 1
- bond_charges: int32 [32, 2], P('grp'), parts along dimension 0, may hold values from 32 to 96, as said below
Outputs:
- new_boundary: bfloat16 [32, 192, 576], P(('grp', 'col'), 'blk'), parts along dimension 0
There are 2 independent parts, one for each index of `grp`. A program takes and returns all parts, laid end to end along the dimension named above; each array names one. Nothing has to cross between parts.
Inputs may be any that keep to these rules, and one draw needn't show every extreme that they name: `bond_charges`: odd counts are 128 minus these, so neither block of a bond holds more than 96 live rows; some bond has an even count of 96 and some bond an odd count of 96. `leg_parity`: [c, 0] is the horizontal leg left of column c, [c, 1] the vertical leg between boundary and row, [c, 2] the outgoing vertical leg.
All inputs are finite; a program needn't handle non-finite values.
Results may differ from a plain program's by a relative error of at most 0.0057.
Values may be sent and summed in bfloat16 or wider, within the bound.
A program may use at most 64 MiB of HBM per device.

v0:
```python
import jax
import jax.numpy as jnp
from jax import lax
from jax.sharding import PartitionSpec as P

CHI = 128
BLOCK = 96
D = 6


def passed_along(x, axis, by):
    length = lax.axis_size(axis)
    return lax.ppermute(x, axis, [(i, (i + by) % length) for i in range(length)])


def live_rows(counts, parity, position):
    limit = jnp.where(parity == 0, counts, CHI - counts)
    return position < limit


def per_device(boundary, row_tensor, left_proj, right_proj, leg_parity, bond_charges):
    col_dev, sub_rows, merged = boundary.shape
    start_col = lax.axis_index("col") * col_dev
    charges_here = lax.dynamic_slice_in_dim(bond_charges, start_col, col_dev, 0)
    charges_next = lax.dynamic_slice_in_dim(jnp.roll(bond_charges, -1, 0), start_col, col_dev, 0)
    legs_here = lax.dynamic_slice_in_dim(leg_parity, start_col, col_dev, 0)
    legs_next = lax.dynamic_slice_in_dim(jnp.roll(leg_parity, -1, 0), start_col, col_dev, 0)
    in_here = charges_here[:, 0]
    out_here = charges_here[:, 1]
    in_next = charges_next[:, 0]
    out_next = charges_next[:, 1]
    left_leg = legs_here[:, 0]
    up_leg = legs_here[:, 1]
    down_leg = legs_here[:, 2]
    right_leg = legs_next[:, 0]
    inside = lax.iota(jnp.int32, BLOCK)
    row_start = lax.axis_index("blk") * sub_rows
    local_index = row_start + lax.iota(jnp.int32, sub_rows)
    local_parity = local_index // BLOCK
    local_position = local_index % BLOCK
    left_sel = (local_parity[None, :, None] + left_leg[:, None, :]) % 2
    left_mask = live_rows(out_here[:, None], local_parity[None, :], local_position[None, :])[
        :, :, None, None
    ] & live_rows(in_here[:, None, None, None], left_sel[..., None], inside[None, None, None, :])
    left_m = left_proj.reshape(col_dev, sub_rows, D, BLOCK) * left_mask.astype(jnp.bfloat16)
    left_dense = jnp.concatenate(
        [
            left_m * (left_sel == 0).astype(jnp.bfloat16)[..., None],
            left_m * (left_sel == 1).astype(jnp.bfloat16)[..., None],
        ],
        axis=3,
    )
    piece = lax.all_gather(boundary, "blk", axis=1, tiled=True)
    count_rows = piece.shape[1]
    row_index = lax.iota(jnp.int32, count_rows)
    row_parity = row_index // BLOCK
    row_position = row_index % BLOCK
    bound_sel = (row_parity[None, :, None] + up_leg[:, None, :]) % 2
    bound_mask = live_rows(in_here[:, None], row_parity[None, :], row_position[None, :])[
        :, :, None, None
    ] & live_rows(in_next[:, None, None, None], bound_sel[..., None], inside[None, None, None, :])
    piece_m = piece.reshape(col_dev, count_rows, D, BLOCK) * bound_mask.astype(jnp.bfloat16)
    absorbed = jnp.einsum(
        "cpla,caub->cplub", left_dense, piece_m, preferred_element_type=jnp.float32
    ).astype(jnp.bfloat16)
    row_keep = (
        left_leg[:, :, None, None, None]
        + up_leg[:, None, :, None, None]
        + down_leg[:, None, None, :, None]
        + right_leg[:, None, None, None, :]
    ) % 2 == 0
    row_sign = 1 - 2 * left_leg[:, :, None, None, None] * up_leg[:, None, :, None, None]
    row_m = row_tensor * jnp.where(row_keep, row_sign, 0).astype(jnp.bfloat16)
    mixed = jnp.einsum("cplub,cludr->cpdrb", absorbed, row_m, preferred_element_type=jnp.float32)
    block_par = (
        local_parity[None, :, None, None] + down_leg[:, None, :, None] + right_leg[:, None, None, :]
    ) % 2
    sign_flip = (1 - 2 * block_par * down_leg[:, None, :, None]).astype(jnp.float32)
    mixed = (mixed * sign_flip[..., None]).astype(jnp.bfloat16)
    mixed_dense = jnp.concatenate(
        [
            mixed * (block_par == 0).astype(jnp.bfloat16)[..., None],
            mixed * (block_par == 1).astype(jnp.bfloat16)[..., None],
        ],
        axis=4,
    )
    incoming = passed_along(right_proj[:1], "col", -1)
    right_next = jnp.concatenate([right_proj[1:], incoming], axis=0)
    piece = lax.all_gather(right_next, "blk", axis=1, tiled=True)
    count_rows = piece.shape[1]
    row_index = lax.iota(jnp.int32, count_rows)
    row_parity = row_index // BLOCK
    row_position = row_index % BLOCK
    right_sel = (row_parity[None, :, None] + right_leg[:, None, :]) % 2
    right_mask = live_rows(in_next[:, None], row_parity[None, :], row_position[None, :])[
        :, :, None, None
    ] & live_rows(out_next[:, None, None, None], right_sel[..., None], inside[None, None, None, :])
    piece_m = piece.reshape(col_dev, count_rows, D, BLOCK) * right_mask.astype(jnp.bfloat16)
    result = jnp.einsum(
        "cpdrb,cbre->cpde", mixed_dense, piece_m, preferred_element_type=jnp.float32
    )
    return result.astype(jnp.bfloat16).reshape(col_dev, sub_rows, merged)


def solution(mesh):
    in_specs = (
        P(("grp", "col"), "blk", None),
        P(("grp", "col"), None, None, None, None),
        P(("grp", "col"), "blk", None),
        P(("grp", "col"), "blk", None),
        P("grp", None, None),
        P("grp", None),
    )
    out_specs = P(("grp", "col"), "blk", None)
    return jax.shard_map(
        per_device, mesh=mesh, in_specs=in_specs, out_specs=out_specs, check_vma=False
    )
```

profile of v0, /device:TPU:0, one launch (start us, length us, event | category | flops | bytes accessed | tf_op | source)
XLA Modules:
  0.0 54.8 jit_solution(14372236034611323243)
XLA Ops:
  0.0 0.8 %slice.62 = bf16[1,48,576]{2,1,0:T(8,128)(2,1)S(1)} slice(bf16[4,48,576]{2,1,0:T(8,128)(2,1)} %param.9), slice={[0:1], [0:48], [0:576]} | slice | bytes 110592 | tf_op jit(solution)/shard_map/slice | solution.py:87
  0.8 5.1 %collective-permute-start = (bf16[1,48,576]{2,1,0:T(8,128)(2,1)S(1)}, bf16[1,48,576]{2,1,0:T(8,128)(2,1)S(1)}, u32[]{:S(2)}, u32[]{:S(2)}) collective-permute-start(bf16[1,48,576]{2,1,0:T(8,128)(2,1)S(1)} %slice.62), channel_id=1, source_target_pairs={{0,12},{4,0},{8,4},{12,8},{1,13},{5,1},{9,5},{13,9},{2,14},{6,2},{... | collective-permute-start | bytes 165896 | tf_op jit(solution)/shard_map/ppermute | solution.py:13
  5.9 0.7 %slice.57 = s32[15,2]{0,1:T(2,128)S(1)} slice(s32[16,2]{0,1:T(2,128)} %param.11), slice={[1:16], [0:2]} | slice | bytes 240 | tf_op jit(solution)/shard_map/jit(_roll_static)/slice | solution.py:25
  6.7 0.8 %pad_add_fusion = s32[16,2]{0,1:T(2,128)S(1)} fusion(s32[1,2]{0,1:T(2,128)} %bitcast.75, s32[15,2]{0,1:T(2,128)S(1)} %slice.57), kind=kLoop, calls=%fused_computation.102 | loop fusion | flops 32 | bytes 256 | tf_op jit(solution)/shard_map/jit(_roll_static)/concatenate | solution.py:25
  7.4 0.8 %constant_dynamic-slice_fusion.2 = (s32[4,2]{0,1:T(2,128)S(1)}, s32[4,2]{0,1:T(2,128)S(1)}) fusion(s32[16,2]{0,1:T(2,128)S(1)} %pad_add_fusion, s32[]{:T(128)S(6)} %select_n.177, s32[16,2]{0,1:T(2,128)} %param.11), kind=kLoop, calls=%fused_computation.97 | loop fusion | bytes 132 | tf_op jit(solution)/shard_map/dynamic_slice | solution.py:25
  8.3 0.8 %slice.51 = s32[15,3,6]{0,2,1:T(8,128)S(1)} slice(s32[16,3,6]{0,2,1:T(8,128)} %param.10), slice={[1:16], [0:3], [0:6]} | slice | bytes 2160 | tf_op jit(solution)/shard_map/jit(_roll_static)/slice | solution.py:27
  9.1 0.8 %constant_dynamic-slice_fusion.1 = (s32[4,1,6]{0,2,1:T(8,128)S(1)}, s32[4,1,6]{0,2,1:T(8,128)S(1)}, s32[4,1,6]{0,2,1:T(8,128)S(1)}, s32[4,1,6]{0,2,1:T(8,128)S(1)}) fusion(s32[16,3,6]{0,2,1:T(8,128)} %param.10, s32[]{:T(128)S(6)} %select_n.177, s32[]{:T(128)S(6)} %add.320, s32[]{:T(128)S(6)} %add.321, s32[1,3,6]{0,2,1:T(8,128)} %bitcast.63, ...), kind=kLoop, calls=%fused_computation.96 | loop fusion | flops 24 | bytes 1836 | tf_op jit(solution)/shard_map/slice | solution.py:32
  9.9 0.1 copy.38
  10.0 0.1 copy.42
  10.1 0.1 copy.39
  10.2 0.1 fusion.45
  10.3 1.3 %reshape.409 = bf16[4,48,6,96]{3,2,1,0:T(8,128)(2,1)S(1)} reshape(bf16[4,48,576]{2,1,0:T(8,128)(2,1)} %param.8) | data formatting | bytes 442368 | tf_op jit(solution)/shard_map/reshape | solution.py:45
  11.6 0.1 copy.44
  11.7 0.1 copy.40
  11.8 1.0 %copy.47 = bf16[4,48,576]{2,0,1:T(4,128)(2,1)S(1)} copy(bf16[4,48,576]{2,1,0:T(8,128)(2,1)} %param.6) | data formatting | bytes 442368 | tf_op args[0]
  12.8 0.0 copy-start
  12.8 9.8 %all_gather.6 = bf16[4,192,576]{2,0,1:T(4,128)(2,1)S(1)} all-gather(bf16[4,48,576]{2,0,1:T(4,128)(2,1)S(1)} %copy.47), channel_id=1, replica_groups=mesh['grp'=2,'col'=4,'blk'=4] {'blk'}, dimensions={1}, use_global_device_ids=true | all-gather | bytes 1105920 | tf_op jit(solution)/shard_map/all_gather | solution.py:53
  22.6 1.3 %copy.48 = bf16[4,192,576]{1,2,0:T(8,128)(2,1)S(1)} copy(bf16[4,192,576]{2,0,1:T(4,128)(2,1)S(1)} %all_gather.6) | data formatting | bytes 1769472 | tf_op jit(solution)/shard_map/all_gather | solution.py:53
  23.9 0.1 copy.45
  24.0 0.1 copy.41
  24.1 0.1 copy.43
  24.2 0.1 broadcast_select_fusion
  24.3 0.4 compare_convert_fusion.1
  24.7 0.4 subtract_convert_fusion
  25.1 0.0 copy-done
  25.1 0.7 %fusion.36 = bf16[4,6,6,6,6,1]{4,0,3,2,1,5:T(4,128)(2,1)S(1)} fusion(bf16[4,6,6,6,6]{4,0,3,2,1:T(4,128)(2,1)S(1)} %copy-done, s32[4,6,6]{0,2,1:T(8,128)S(1)} %get-tuple-element.15, s32[4,6]{1,0:T(4,128)S(1)} %bitcast.66, s32[4,6,6,6]{0,3,2,1:T(8,128)S(1)} %broadcast_add_fusion), kind=kLoop, calls=%fused_computation.52 | loop fusion | flops 98496 | bytes 24864 | tf_op jit(solution)/shard_map/mul | solution.py:73
  25.8 0.1 select_compare_fusion.2
  25.9 0.1 fusion.41
  26.0 0.1 select_compare_fusion
  26.1 0.6 %broadcast_multiply_fusion.3 = (bf16[4,48,6,96]{3,1,2,0:T(8,128)(2,1)S(1)}, bf16[4,48,6,96]{3,1,2,0:T(8,128)(2,1)S(1)}) fusion(bf16[4,48,6]{1,2,0:T(8,128)(2,1)S(1)} %get-tuple-element.16, bf16[4,48,6,96]{3,2,1,0:T(8,128)(2,1)S(1)} %reshape.409, s32[4,48,6]{1,2,0:T(8,128)S(1)} %get-tuple-element.31, pred[4,48]{1,0:T(4,128)(4,1)S(1)} %select_compare_fusion.2, ...), kind=kLoop, calls=%fused_computation.54 | loop fusion | flops 1105920 | bytes 672960 | tf_op jit(solution)/shard_map/mul | solution.py:48
  26.7 1.0 %convert_bitcast_fusion = bf16[4,48,6,6,96,1]{4,1,3,2,0,5:T(8,128)(2,1)S(1)} fusion(bf16[4,192,6,96]{1,3,2,0:T(8,128)(2,1)S(1)} %bitcast.61, s32[4,192,6]{1,2,0:T(8,128)S(1)} %get-tuple-element.24, pred[4,192]{1,0:T(4,128)(4,1)S(1)} %get-tuple-element.19, bf16[4,48,6,96]{3,1,2,0:T(8,128)(2,1)S(1)} %get-tuple-element.8, ...), kind=kOutput, calls=%fused_computation.13 | convolution fusion | flops 257679360 | bytes 2673408 | tf_op jit(solution)/shard_map/cpla,caub->cplub/dot_general | solution.py:63
  27.7 6.6 %broadcast_multiply_fusion.1 = (bf16[4,48,6,6,96]{4,3,1,2,0:T(8,128)(2,1)S(1)}, bf16[4,48,6,6,96]{4,3,1,2,0:T(8,128)(2,1)S(1)}) fusion(bf16[4,48,6,6]{3,1,2,0:T(8,128)(2,1)S(1)} %get-tuple-element.9, bf16[4,48,6,6]{3,1,2,0:T(8,128)(2,1)S(1)} %get-tuple-element.10, f32[4,48,6,6]{3,1,2,0:T(8,128)S(1)} %subtract_convert_fusion, ...), kind=kOutput, calls=%fused_computation.20 | convolution fusion | flops 50429952 | bytes 4046976 | tf_op jit(solution)/shard_map/cplub,cludr->cpdrb/dot_general | solution.py:74
  34.3 0.0 slice-start
  34.3 4.5 %pad_maximum_fusion = bf16[4,48,6,6,192]{4,3,1,2,0:T(8,128)(2,1)} fusion(bf16[4,48,6,6,96]{4,3,1,2,0:T(8,128)(2,1)S(1)} %get-tuple-element.6, bf16[4,48,6,6,96]{4,3,1,2,0:T(8,128)(2,1)S(1)} %get-tuple-element.5), kind=kLoop, calls=%fused_computation | loop fusion | flops 5308416 | bytes 5308416 | tf_op jit(solution)/shard_map/concatenate | solution.py:80
  38.8 0.0 collective-permute-done
  38.8 0.0 slice-done
  38.9 0.1 copy.52
  39.0 9.8 %all_gather.7 = bf16[4,192,576]{2,0,1:T(4,128)(2,1)S(1)} all-gather(bf16[4,48,576]{2,0,1:T(4,128)(2,1)S(1)} %copy.52), channel_id=1, replica_groups=mesh['grp'=2,'col'=4,'blk'=4] {'blk'}, dimensions={1}, use_global_device_ids=true | all-gather | bytes 1105920 | tf_op jit(solution)/shard_map/all_gather | solution.py:89
  48.7 1.3 %copy.53 = bf16[4,192,576]{1,2,0:T(8,128)(2,1)S(1)} copy(bf16[4,192,576]{2,0,1:T(4,128)(2,1)S(1)} %all_gather.7) | data formatting | bytes 1769472 | tf_op jit(solution)/shard_map/all_gather | solution.py:89
  50.0 3.7 %fusion.14 = bf16[4,48,6,96]{3,1,2,0:T(8,128)(2,1)S(1)} fusion(bf16[4,48,6,6,192]{4,3,1,2,0:T(8,128)(2,1)} %pad_maximum_fusion, bf16[4,192,6,96]{1,3,2,0:T(8,128)(2,1)S(1)} %bitcast.62, s32[4,192,6]{1,2,0:T(8,128)S(1)} %get-tuple-element.23, pred[4,192]{1,0:T(4,128)(4,1)S(1)} %get-tuple-element.18), kind=kOutput, calls=%fused_computation.15 | convolution fusion | flops 256241664 | bytes 3779328 | tf_op jit(solution)/shard_map/cpdrb,cbre->cpde/dot_general | solution.py:99
  53.7 0.1 copy.56
  53.8 1.0 %reshape.412 = bf16[4,48,576]{2,1,0:T(8,128)(2,1)} reshape(bf16[4,48,6,96]{3,2,1,0:T(8,128)(2,1)S(1)} %copy.56) | data formatting | bytes 442368 | tf_op jit(solution)/shard_map/reshape | solution.py:102
  (13 shorter events, 0.1 us)
Async XLA Ops:
  0.8 38.0 %collective-permute-start = (bf16[1,48,576]{2,1,0:T(8,128)(2,1)S(1)}, bf16[1,48,576]{2,1,0:T(8,128)(2,1)S(1)}, u32[]{:S(2)}, u32[]{:S(2)}) collective-permute-start(bf16[1,48,576]{2,1,0:T(8,128)(2,1)S(1)} %slice.62), channel_id=1, source_target_pairs={{0,12},{4,0},{8,4},{12,8},{1,13},{5,1},{9,5},{13,9},{2,14},{6,2},{... | collective-permute-start | bytes 165896 | tf_op jit(solution)/shard_map/ppermute | solution.py:13
  12.8 12.3 %copy-start = (bf16[4,6,6,6,6]{4,0,3,2,1:T(4,128)(2,1)S(1)}, bf16[4,6,6,6,6]{4,0,3,2,1:T(4,128)(2,1)}, u32[]{:S(2)}) copy-start(bf16[4,6,6,6,6]{4,0,3,2,1:T(4,128)(2,1)} %param.7) | copy-start | bytes 31108
  34.3 4.5 %slice-start = ((bf16[4,48,576]{2,1,0:T(8,128)(2,1)}), bf16[3,48,576]{2,1,0:T(8,128)(2,1)S(1)}, s32[]{:S(2)}) async-start(bf16[4,48,576]{2,1,0:T(8,128)(2,1)} %param.9), calls=%async_computation | async-start | bytes 368640 | tf_op jit(solution)/shard_map/slice | solution.py:88
where the time goes:
time: 55.2 us; the launch traced here: 54.8 us
  blocking collectives  19.6 us (36%)
  matrix products  11.3 us (20%)
  local copies, waits for them, and re-layouts  9.95 us (18%)
  other arithmetic  8.7 us (16%)
  starting transfers between devices  5.08 us (9%)
    all_gather x1, blocking collectives, per_device(): piece = lax.all_gather(boundary, 'blk', axis=1, tiled=True)  9.8 us
    all_gather x1, blocking collectives, per_device(): piece = lax.all_gather(right_next, 'blk', axis=1, tiled=True)  9.78 us
    dot_general x1, matrix products, per_device(): jnp.einsum('cplub,cludr->cpdrb', absorbed, row_m, preferred_element_type=...  6.63 us
    ppermute x1, starting transfers between devices, passed_along(): lax.ppermute(x, axis, [(i, (i + by) % length) for i in range(length)])  5.08 us
    concatenate x1, other arithmetic, per_device(): jnp.concatenate([mixed * (block_par == 0).astype(jnp.bfloat16)[..., None]...  4.46 us
    dot_general x1, matrix products, per_device(): jnp.einsum('cpdrb,cbre->cpde', mixed_dense, piece_m, preferred_element_ty...  3.67 us
    reshape x1, local copies, waits for them, and re-layouts, per_device(): left_proj.reshape(col_dev, sub_rows, D, BLOCK)  1.31 us
    all_gather x1, local copies, waits for them, and re-layouts, per_device(): piece = lax.all_gather(boundary, 'blk', axis=1, tiled=True)  1.27 us
  transfers between devices with their start and end apart: 1, of which 0 were waited for; matrix products, arithmetic and copies ran while one was open for 42% of the time, Pallas kernels for 0%

commit v1 on v0

v1 whole, which is shorter than its diff:
```python
import functools

import jax
import jax.numpy as jnp
from jax import lax
from jax.experimental import pallas as pl
from jax.experimental.pallas import tpu as pltpu
from jax.sharding import PartitionSpec as P

CHI = 128
BLOCK = 96
D = 6
LANES = 128
SUB = 8
KRON = D * D * SUB
MESH = pl.DeviceIdType.MESH


def limit_of(count, parity):
    return jnp.where(parity == 0, count, CHI - count)


def pick(index, scalars):
    acc = jnp.zeros(index.shape, jnp.int32)
    for at, value in enumerate(scalars):
        acc = jnp.where(index == at, value, acc)
    return acc


def kernel(
    cols, subs, n_blk, n_col,
    bound_hbm, row_hbm, left_hbm, right_hbm, legs, charges, out_ref,
    bound_all, right_all, left_own, row_own, left_dense, kron, bound_pad, right_pad,
    local_sem, send_sem, recv_sem, z_sem,
):
    me = lax.axis_index("blk")
    here = lax.axis_index("col")
    partner = me + 1 - 2 * (me % 2)
    across = (me + 2) % n_blk
    across_partner = (partner + 2) % n_blk
    col_left = (here + n_col - 1) % n_col
    col_right = (here + 1) % n_col
    all_cols = cols * n_col
    parity = me // 2
    row_base = (me % 2) * subs

    own_copies = [
        pltpu.make_async_copy(bound_hbm, bound_all.at[me], local_sem.at[0]),
        pltpu.make_async_copy(
            right_hbm.at[pl.ds(1, cols - 1)], right_all.at[me, pl.ds(0, cols - 1)], local_sem.at[1]
        ),
        pltpu.make_async_copy(left_hbm, left_own, local_sem.at[2]),
        pltpu.make_async_copy(row_hbm, row_own, local_sem.at[3]),
    ]
    for copy in own_copies:
        copy.start()

    barrier = pltpu.get_barrier_semaphore()
    for target in ({"blk": partner}, {"blk": across}, {"col": col_left}, {"col": col_right}):
        pl.semaphore_signal(barrier, inc=1, device_id=target, device_id_type=MESH)
    pl.semaphore_wait(barrier, 4)

    def z_copy():
        return pltpu.make_async_remote_copy(
            src_ref=right_hbm.at[0], dst_ref=right_all.at[me, cols - 1],
            send_sem=z_sem.at[0], recv_sem=z_sem.at[1],
            device_id={"col": col_left}, device_id_type=MESH,
        )

    def link(which, route, c):
        buffer = bound_all if which == 0 else right_all
        slot = across if route == 2 else me
        target = across if route == 0 else partner
        return pltpu.make_async_remote_copy(
            src_ref=buffer.at[slot, c], dst_ref=buffer.at[slot, c],
            send_sem=send_sem.at[which, route, c], recv_sem=recv_sem.at[which, route, c],
            device_id={"blk": target}, device_id_type=MESH,
        )

    z_copy().start()
    own_copies[0].wait()
    link(0, 0, 0).start()
    own_copies[1].wait()
    for c in range(cols):
        if c > 0:
            link(0, 0, c).start()
        if c < cols - 1:
            link(1, 0, c).start()
    for c in range(cols):
        link(0, 1, c).start()
        if c < cols - 1:
            link(1, 1, c).start()
    own_copies[2].wait()
    own_copies[3].wait()

    bound_pad[...] = jnp.zeros_like(bound_pad)
    right_pad[...] = jnp.zeros_like(right_pad)
    left_dense[...] = jnp.zeros_like(left_dense)

    z_copy().wait_recv()
    link(1, 0, cols - 1).start()
    link(1, 1, cols - 1).start()

    def scalars(c):
        at = here * cols + c
        nxt = (at + 1) % all_cols
        p0 = [legs[at, 0, k] for k in range(D)]
        p1 = [legs[at, 1, k] for k in range(D)]
        p2 = [legs[at, 2, k] for k in range(D)]
        pr = [legs[nxt, 0, k] for k in range(D)]
        return p0, p1, p2, pr, charges[at, 0], charges[at, 1], charges[nxt, 0], charges[nxt, 1]

    lane96 = lax.broadcasted_iota(jnp.int32, (subs, BLOCK), 1)
    row96 = lax.broadcasted_iota(jnp.int32, (subs, BLOCK), 0)

    def as_mask(condition):
        return jnp.where(condition, 1.0, 0.0)

    def prepare(c, _):
        p0, p1, p2, pr, in_here, out_here, in_next, out_next = scalars(c)
        for l in range(D):
            q = (parity + p0[l]) % 2
            segment = left_own[c, :, l * BLOCK:(l + 1) * BLOCK]
            keep = lane96 < limit_of(in_here, q)
            even = as_mask(keep & (q == 0)).astype(jnp.bfloat16)
            odd = as_mask(keep & (q == 1)).astype(jnp.bfloat16)
            left_dense[c, l * subs:(l + 1) * subs, 0:BLOCK] = segment * even
            left_dense[c, l * subs:(l + 1) * subs, LANES:LANES + BLOCK] = segment * odd
        w = row_own[c].astype(jnp.float32).reshape(D * D, D, D)
        w = jnp.concatenate([w, jnp.zeros((D * D, SUB - D, D), jnp.float32)], axis=1)
        w = w.reshape(KRON, D).astype(jnp.bfloat16)
        spread_row = lax.broadcasted_iota(jnp.int32, (KRON, D), 0)
        spread_lane = lax.broadcasted_iota(jnp.int32, (KRON, D), 1)
        spread = as_mask((spread_row // SUB) % D == spread_lane).astype(jnp.bfloat16)
        big = lax.dot_general(
            spread, w, (((1,), (1,)), ((), ())), preferred_element_type=jnp.float32
        )
        row = lax.broadcasted_iota(jnp.int32, (KRON, KRON), 0)
        lane = lax.broadcasted_iota(jnp.int32, (KRON, KRON), 1)
        big = jnp.where(row // (D * SUB) == lane % SUB, big, 0.0).astype(jnp.bfloat16)
        group = as_mask(row // SUB == lane // SUB).astype(jnp.bfloat16)
        big = jnp.dot(big, group, preferred_element_type=jnp.float32)
        rows = lax.broadcasted_iota(jnp.int32, (KRON, 1), 0)
        lanes = lax.broadcasted_iota(jnp.int32, (1, KRON), 1)
        down = pick(rows // (D * SUB), p2)
        right = pick((rows // SUB) % D, pr)
        left = pick(lanes // (D * SUB), p0)
        up = pick((lanes // SUB) % D, p1)
        row_sign = 1 - 2 * (((parity + down + right) % 2) * down)
        lane_sign = 1 - 2 * left * up
        row_par = (down + right) % 2
        lane_par = (left + up) % 2
        same = row_par * lane_par + (1 - row_par) * (1 - lane_par)
        factor = (same * row_sign * lane_sign).astype(jnp.float32)
        kron[c] = jnp.where(row % SUB == lane % SUB, big * factor, 0.0).astype(jnp.bfloat16)
        return _

    lax.fori_loop(0, cols, prepare, 0)

    def column(c, _):
        p0, p1, p2, pr, in_here, out_here, in_next, out_next = scalars(c)
        link(0, 0, c).wait_recv()
        link(0, 2, c).start()
        link(0, 1, c).wait_recv()
        link(0, 2, c).wait_recv()
        for slot in range(n_blk):
            top = (slot // 2) * LANES + (slot % 2) * subs
            for u in range(D):
                bound_pad[top:top + subs, u * LANES:u * LANES + BLOCK] = bound_all[
                    slot, c, :, u * BLOCK:(u + 1) * BLOCK
                ]
        absorbed = jnp.dot(left_dense[c], bound_pad[...], preferred_element_type=jnp.float32)
        high = subs // SUB
        x = jnp.concatenate(
            [
                jnp.concatenate(
                    [
                        absorbed[l * subs + h * SUB:l * subs + (h + 1) * SUB, u * LANES:(u + 1) * LANES]
                        for h in range(high)
                    ],
                    axis=1,
                )
                for l in range(D)
                for u in range(D)
            ],
            axis=0,
        ).astype(jnp.bfloat16)
        mixed = jnp.dot(kron[c], x, preferred_element_type=jnp.float32)
        y = jnp.concatenate(
            [
                jnp.concatenate(
                    [
                        mixed[(d * D + r) * SUB:(d * D + r + 1) * SUB, h * LANES:(h + 1) * LANES]
                        for r in range(D)
                    ],
                    axis=1,
                )
                for d in range(D)
                for h in range(high)
            ],
            axis=0,
        ).astype(jnp.bfloat16)

        link(1, 0, c).wait_recv()
        link(1, 2, c).start()
        link(1, 1, c).wait_recv()
        link(1, 2, c).wait_recv()
        for half in range(2):
            even_live = as_mask(row96 + half * subs < in_next).astype(jnp.bfloat16)
            odd_live = as_mask(row96 + half * subs < CHI - in_next).astype(jnp.bfloat16)
            for r in range(D):
                span = slice(r * BLOCK, (r + 1) * BLOCK)
                even = right_all[half, c, :, span] * even_live
                odd = right_all[2 + half, c, :, span] * odd_live
                straight = (parity + pr[r]) % 2 == 0
                top = r * LANES + half * subs
                right_pad[top:top + subs, 0:BLOCK] = jnp.where(straight, even, odd)
                right_pad[top:top + subs, LANES:LANES + BLOCK] = jnp.where(straight, odd, even)
        result = jnp.dot(y, right_pad[...], preferred_element_type=jnp.float32)
        row_live = row96 + row_base < limit_of(out_here, parity)
        for d in range(D):
            rows = slice(d * subs, (d + 1) * subs)
            part = jnp.where(p2[d] == 0, result[rows, 0:BLOCK], result[rows, LANES:LANES + BLOCK])
            live = row_live & (lane96 < limit_of(out_next, (parity + p2[d]) % 2))
            out_ref[c, :, d * BLOCK:(d + 1) * BLOCK] = jnp.where(live, part, 0.0).astype(jnp.bfloat16)
        return _

    lax.fori_loop(0, cols, column, 0)

    z_copy().wait_send()
    for c in range(cols):
        for which in range(2):
            for route in range(3):
                link(which, route, c).wait_send()


def per_device(n_blk, n_col, boundary, row_tensor, left_proj, right_proj, leg_parity, bond_charges):
    cols, subs, merged = boundary.shape
    bf16 = jnp.bfloat16
    hbm = pl.BlockSpec(memory_space=pl.ANY)
    smem = pl.BlockSpec(memory_space=pltpu.SMEM)
    return pl.pallas_call(
        functools.partial(kernel, cols, subs, n_blk, n_col),
        out_shape=jax.ShapeDtypeStruct(boundary.shape, bf16),
        in_specs=[hbm, hbm, hbm, hbm, smem, smem],
        out_specs=pl.BlockSpec(memory_space=pltpu.VMEM),
        scratch_shapes=[
            pltpu.VMEM((n_blk, cols, subs, merged), bf16),
            pltpu.VMEM((n_blk, cols, subs, merged), bf16),
            pltpu.VMEM((cols, subs, merged), bf16),
            pltpu.VMEM(row_tensor.shape, bf16),
            pltpu.VMEM((cols, D * subs, 2 * LANES), bf16),
            pltpu.VMEM((cols, KRON, KRON), bf16),
            pltpu.VMEM((2 * LANES, D * LANES), bf16),
            pltpu.VMEM((D * LANES, 2 * LANES), bf16),
            pltpu.SemaphoreType.DMA((4,)),
            pltpu.SemaphoreType.DMA((2, 3, cols)),
            pltpu.SemaphoreType.DMA((2, 3, cols)),
            pltpu.SemaphoreType.DMA((2,)),
        ],
        compiler_params=pltpu.CompilerParams(
            collective_id=0, has_side_effects=True, vmem_limit_bytes=48 * 1024 * 1024
        ),
    )(boundary, row_tensor, left_proj, right_proj, leg_parity, bond_charges)


def solution(mesh):
    in_specs = (
        P(("grp", "col"), "blk", None),
        P(("grp", "col"), None, None, None, None),
        P(("grp", "col"), "blk", None),
        P(("grp", "col"), "blk", None),
        P("grp", None, None),
        P("grp", None),
    )
    out_specs = P(("grp", "col"), "blk", None)
    body = functools.partial(per_device, mesh.shape["blk"], mesh.shape["col"])
    return jax.shard_map(body, mesh=mesh, in_specs=in_specs, out_specs=out_specs, check_vma=False)
```

time: 55.2 us -> 30.5 us (0.55)
  Pallas kernels: 0 us -> 25.9 us
  blocking collectives: 19.6 us -> 0 us
  matrix products: 11.3 us -> 0 us
  other arithmetic: 8.7 us -> 0 us
  local copies, waits for them, and re-layouts: 9.95 us -> 4.34 us
  starting transfers between devices: 5.08 us -> 0 us
    pallas_call x0 -> x1, Pallas kernels: none -> 25.9 us  [per_device(): pl.pallas_call(functools.partial(kernel, cols, subs, n_blk, n_col), out_s...]
    all_gather x2 -> x0, blocking collectives: 19.6 us -> none  [the longest x1 9.8 us: per_device(): piece = lax.all_gather(boundary, 'blk', axis=1, tiled=True)]
    dot_general x3 -> x0, matrix products: 11.3 us -> none  [the longest x1 6.63 us: per_device(): jnp.einsum('cplub,cludr->cpdrb', absorbed, row_m, preferred_element_type=...]
    concatenate x3 -> x0, other arithmetic: 5.25 us -> none  [the longest x1 4.46 us: per_device(): jnp.concatenate([mixed * (block_par == 0).astype(jnp.bfloat16)[..., None]...]
    ppermute x1 -> x0, starting transfers between devices: 5.08 us -> none  [passed_along(): lax.ppermute(x, axis, [(i, (i + by) % length) for i in range(length)])]
    unnamed x3 -> x10, local copies, waits for them, and re-layouts: 1.05 us -> 4.34 us
    slice x9 -> x0, local copies, waits for them, and re-layouts: 2.74 us -> none  [the longest x1 0.83 us: per_device(): incoming = passed_along(right_proj[:1], 'col', -1)]
    all_gather x2 -> x0, local copies, waits for them, and re-layouts: 2.55 us -> none  [the longest x1 1.27 us: per_device(): piece = lax.all_gather(boundary, 'blk', axis=1, tiled=True)]
  transfers between devices with their start and end apart: 1 -> 0, of which waited for: 0 -> 0; matrix products, arithmetic and copies ran while one was open for 42% -> 0% of each run, Pallas kernels for 0% -> 0%
where the time goes in v1:
time: 30.5 us; the launch traced here: 30.2 us
  Pallas kernels  25.9 us (85%)
  local copies, waits for them, and re-layouts  4.34 us (14%)
    pallas_call x1, Pallas kernels, per_device(): pl.pallas_call(functools.partial(kernel, cols, subs, n_blk, n_col), out_s...  25.9 us
    unnamed x10, local copies, waits for them, and re-layouts  4.34 us

profile of v1, /device:TPU:0, one launch (start us, length us, event | category | flops | bytes accessed | tf_op | source)
XLA Modules:
  0.0 30.2 jit_solution(10033757340878252414)
XLA Ops:
  0.0 0.8 %copy.9.charges = s32[16,2]{1,0:T(8,128)S(1)} copy(s32[16,2]{0,1:T(2,128)} %param.11) | data formatting | bytes 256 | tf_op args[5]
  0.8 0.8 %copy.8.legs = s32[16,3,6]{2,1,0:T(4,128)S(1)} copy(s32[16,3,6]{0,2,1:T(8,128)} %param.10) | data formatting | bytes 2304 | tf_op args[4]
  1.6 0.0 copy-start
  1.6 0.0 copy-start.1
  1.6 1.1 %copy.7.row_hbm = bf16[4,6,6,6,6]{4,3,2,1,0:T(8,128)(2,1)S(1)} copy(bf16[4,6,6,6,6]{4,0,3,2,1:T(4,128)(2,1)} %param.7) | data formatting | bytes 20736 | tf_op args[1]
  2.6 0.0 copy-done
  2.6 0.1 copy-done.1
  2.7 0.0 copy-start.2
  2.7 0.9 %copy-done.2 = bf16[4,48,576]{2,1,0:T(8,128)(2,1)S(1)} copy-done((bf16[4,48,576]{2,1,0:T(8,128)(2,1)S(1)}, bf16[4,48,576]{2,1,0:T(8,128)(2,1)}, u32[]{:S(2)}) %copy-start.2) | copy-done | bytes 221208
  3.7 25.9 %shard_map.64 = bf16[4,48,576]{2,1,0:T(8,128)(2,1)S(1)} custom-call(bf16[4,48,576]{2,1,0:T(8,128)(2,1)S(1)} %copy-done, bf16[4,6,6,6,6]{4,3,2,1,0:T(8,128)(2,1)S(1)} %copy.7.row_hbm, bf16[4,48,576]{2,1,0:T(8,128)(2,1)S(1)} %copy-done.1, bf16[4,48,576]{2,1,0:T(8,128)(2,1)S(1)} %copy-done.2, s32[16,3,6]{2,1,0:T(4,128)S(1)} %copy.8.legs, s32[16,2]{1,0:T(8,128)S(1)} %copy.9.charges), custom_call_target="tpu_custom_call" | custom-call | tf_op jit(solution)/shard_map/pallas_call | solution.py:242
  29.5 0.7 %copy.11 = bf16[4,48,576]{2,1,0:T(8,128)(2,1)} copy(bf16[4,48,576]{2,1,0:T(8,128)(2,1)S(1)} %shard_map.64) | data formatting | bytes 442368
Async XLA Ops:
  1.6 1.1 %copy-start = (bf16[4,48,576]{2,1,0:T(8,128)(2,1)S(1)}, bf16[4,48,576]{2,1,0:T(8,128)(2,1)}, u32[]{:S(2)}) copy-start(bf16[4,48,576]{2,1,0:T(8,128)(2,1)} %bound_hbm.1) | copy-start | bytes 663556
  1.6 1.2 %copy-start.1 = (bf16[4,48,576]{2,1,0:T(8,128)(2,1)S(1)}, bf16[4,48,576]{2,1,0:T(8,128)(2,1)}, u32[]{:S(2)}) copy-start(bf16[4,48,576]{2,1,0:T(8,128)(2,1)} %left_hbm.1) | copy-start | bytes 663556
  2.7 0.9 %copy-start.2 = (bf16[4,48,576]{2,1,0:T(8,128)(2,1)S(1)}, bf16[4,48,576]{2,1,0:T(8,128)(2,1)}, u32[]{:S(2)}) copy-start(bf16[4,48,576]{2,1,0:T(8,128)(2,1)} %right_hbm.1) | copy-start | bytes 663556

commit v2 on v1

--- a/solution.py
+++ b/solution.py
@@ -30,7 +30,7 @@
 def kernel(
     cols, subs, n_blk, n_col,
     bound_hbm, row_hbm, left_hbm, right_hbm, legs, charges, out_ref,
-    bound_all, right_all, left_own, row_own, left_dense, kron, bound_pad, right_pad,
+    bound_all, right_all, left_own, row_own, row_wide, left_dense, kron, bound_pad, right_pad,
     local_sem, send_sem, recv_sem, z_sem,
 ):
     me = lax.axis_index("blk")
@@ -104,11 +104,11 @@
     def scalars(c):
         at = here * cols + c
         nxt = (at + 1) % all_cols
-        p0 = [legs[at, 0, k] for k in range(D)]
-        p1 = [legs[at, 1, k] for k in range(D)]
-        p2 = [legs[at, 2, k] for k in range(D)]
-        pr = [legs[nxt, 0, k] for k in range(D)]
-        return p0, p1, p2, pr, charges[at, 0], charges[at, 1], charges[nxt, 0], charges[nxt, 1]
+        p0 = [legs[0, k, at] for k in range(D)]
+        p1 = [legs[1, k, at] for k in range(D)]
+        p2 = [legs[2, k, at] for k in range(D)]
+        pr = [legs[0, k, nxt] for k in range(D)]
+        return p0, p1, p2, pr, charges[0, at], charges[1, at], charges[0, nxt], charges[1, nxt]
 
     lane96 = lax.broadcasted_iota(jnp.int32, (subs, BLOCK), 1)
     row96 = lax.broadcasted_iota(jnp.int32, (subs, BLOCK), 0)
@@ -126,9 +126,7 @@
             odd = as_mask(keep & (q == 1)).astype(jnp.bfloat16)
             left_dense[c, l * subs:(l + 1) * subs, 0:BLOCK] = segment * even
             left_dense[c, l * subs:(l + 1) * subs, LANES:LANES + BLOCK] = segment * odd
-        w = row_own[c].astype(jnp.float32).reshape(D * D, D, D)
-        w = jnp.concatenate([w, jnp.zeros((D * D, SUB - D, D), jnp.float32)], axis=1)
-        w = w.reshape(KRON, D).astype(jnp.bfloat16)
+        w = row_wide[pl.ds(c, D * D * D, stride=cols), :][:, 0:D].astype(jnp.bfloat16)
         spread_row = lax.broadcasted_iota(jnp.int32, (KRON, D), 0)
         spread_lane = lax.broadcasted_iota(jnp.int32, (KRON, D), 1)
         spread = as_mask((spread_row // SUB) % D == spread_lane).astype(jnp.bfloat16)
@@ -137,8 +135,12 @@
         )
         row = lax.broadcasted_iota(jnp.int32, (KRON, KRON), 0)
         lane = lax.broadcasted_iota(jnp.int32, (KRON, KRON), 1)
-        big = jnp.where(row // (D * SUB) == lane % SUB, big, 0.0).astype(jnp.bfloat16)
-        group = as_mask(row // SUB == lane // SUB).astype(jnp.bfloat16)
+        flat_row = lax.broadcasted_iota(jnp.int32, (KRON, D * D * D), 0)
+        flat_lane = lax.broadcasted_iota(jnp.int32, (KRON, D * D * D), 1)
+        big = jnp.where(flat_row // (D * SUB) == flat_lane % D, big, 0.0).astype(jnp.bfloat16)
+        group_row = lax.broadcasted_iota(jnp.int32, (D * D * D, KRON), 0)
+        group_lane = lax.broadcasted_iota(jnp.int32, (D * D * D, KRON), 1)
+        group = as_mask(group_row // D == group_lane // SUB).astype(jnp.bfloat16)
         big = jnp.dot(big, group, preferred_element_type=jnp.float32)
         rows = lax.broadcasted_iota(jnp.int32, (KRON, 1), 0)
         lanes = lax.broadcasted_iota(jnp.int32, (1, KRON), 1)
@@ -155,6 +157,7 @@
         kron[c] = jnp.where(row % SUB == lane % SUB, big * factor, 0.0).astype(jnp.bfloat16)
         return _
 
+    row_wide[:, 0:D] = row_own[...].astype(jnp.float32)
     lax.fori_loop(0, cols, prepare, 0)
 
     def column(c, _):
@@ -237,6 +240,7 @@
 def per_device(n_blk, n_col, boundary, row_tensor, left_proj, right_proj, leg_parity, bond_charges):
     cols, subs, merged = boundary.shape
     bf16 = jnp.bfloat16
+    row_flat = row_tensor.transpose(1, 2, 3, 0, 4).reshape(D * D * D * cols, D)
     hbm = pl.BlockSpec(memory_space=pl.ANY)
     smem = pl.BlockSpec(memory_space=pltpu.SMEM)
     return pl.pallas_call(
@@ -248,7 +252,8 @@
             pltpu.VMEM((n_blk, cols, subs, merged), bf16),
             pltpu.VMEM((n_blk, cols, subs, merged), bf16),
             pltpu.VMEM((cols, subs, merged), bf16),
-            pltpu.VMEM(row_tensor.shape, bf16),
+            pltpu.VMEM(row_flat.shape, bf16),
+            pltpu.VMEM((row_flat.shape[0], LANES), jnp.float32),
             pltpu.VMEM((cols, D * subs, 2 * LANES), bf16),
             pltpu.VMEM((cols, KRON, KRON), bf16),
             pltpu.VMEM((2 * LANES, D * LANES), bf16),
@@ -259,9 +264,9 @@
             pltpu.SemaphoreType.DMA((2,)),
         ],
         compiler_params=pltpu.CompilerParams(
-            collective_id=0, has_side_effects=True, vmem_limit_bytes=48 * 1024 * 1024
+            collective_id=0, has_side_effects=True
         ),
-    )(boundary, row_tensor, left_proj, right_proj, leg_parity, bond_charges)
+    )(boundary, row_flat, left_proj, right_proj, leg_parity.transpose(1, 2, 0), bond_charges.T)
 
 
 def solution(mesh):

time: 30.5 us -> 27.5 us (0.902)
  local copies, waits for them, and re-layouts: 4.34 us -> 1.66 us
    unnamed x10 -> x1, local copies, waits for them, and re-layouts: 4.34 us -> 1.66 us
where the time goes in v2:
time: 27.5 us; the launch traced here: 27.2 us
  Pallas kernels  25.6 us (93%)
  local copies, waits for them, and re-layouts  1.66 us (6%)
    pallas_call x1, Pallas kernels, per_device(): pl.pallas_call(functools.partial(kernel, cols, subs, n_blk, n_col), out_s...  25.6 us
    unnamed x1, local copies, waits for them, and re-layouts  1.66 us

profile of v2, /device:TPU:0, one launch (start us, length us, event | category | flops | bytes accessed | tf_op | source)
XLA Modules:
  0.0 27.2 jit_solution(7790008189871422066)
XLA Ops:
  0.0 25.6 %shard_map.64 = bf16[4,48,576]{2,1,0:T(8,128)(2,1)} custom-call(bf16[4,48,576]{2,1,0:T(8,128)(2,1)} %bound_hbm.1, bf16[864,6]{1,0:T(8,128)(2,1)} %bitcast.5, bf16[4,48,576]{2,1,0:T(8,128)(2,1)} %left_hbm.1, bf16[4,48,576]{2,1,0:T(8,128)(2,1)} %right_hbm.1, s32[3,6,16]{2,1,0:T(8,128)} %bitcast.6, s32[2,16]{1,0:T(2,128)} %bitcast.7), custom_call_target="tpu_custom_call" | custom-call | tf_op jit(solution)/shard_map/pallas_call | solution.py:246
  25.6 1.7 %copy.8 = bf16[4,48,576]{2,1,0:T(8,128)(2,1)} copy(bf16[4,48,576]{2,1,0:T(8,128)(2,1)} %shard_map.64) | data formatting | bytes 442368

commit v3 on v2

--- a/solution.py
+++ b/solution.py
@@ -30,8 +30,8 @@
 def kernel(
     cols, subs, n_blk, n_col,
     bound_hbm, row_hbm, left_hbm, right_hbm, legs, charges, out_ref,
-    bound_all, right_all, left_own, row_own, row_wide, left_dense, kron, bound_pad, right_pad,
-    local_sem, send_sem, recv_sem, z_sem,
+    bound_all, right_all, left_own, row_own, row_wide, left_dense, kron, bound_pad, right_pad, y_ref, out_own,
+    local_sem, send_sem, recv_sem, z_sem, out_sem,
 ):
     me = lax.axis_index("blk")
     here = lax.axis_index("col")
@@ -58,6 +58,9 @@
     barrier = pltpu.get_barrier_semaphore()
     for target in ({"blk": partner}, {"blk": across}, {"col": col_left}, {"col": col_right}):
         pl.semaphore_signal(barrier, inc=1, device_id=target, device_id_type=MESH)
+    bound_pad[...] = jnp.zeros_like(bound_pad)
+    right_pad[...] = jnp.zeros_like(right_pad)
+    left_dense[...] = jnp.zeros_like(left_dense)
     pl.semaphore_wait(barrier, 4)
 
     def z_copy():
@@ -92,10 +95,6 @@
             link(1, 1, c).start()
     own_copies[2].wait()
     own_copies[3].wait()
-
-    bound_pad[...] = jnp.zeros_like(bound_pad)
-    right_pad[...] = jnp.zeros_like(right_pad)
-    left_dense[...] = jnp.zeros_like(left_dense)
 
     z_copy().wait_recv()
     link(1, 0, cols - 1).start()
@@ -160,10 +159,13 @@
     row_wide[:, 0:D] = row_own[...].astype(jnp.float32)
     lax.fori_loop(0, cols, prepare, 0)
 
+    def out_copy(c):
+        return pltpu.make_async_copy(out_own.at[c], out_ref.at[c], out_sem.at[c])
+
     def column(c, _):
         p0, p1, p2, pr, in_here, out_here, in_next, out_next = scalars(c)
-        link(0, 0, c).wait_recv()
-        link(0, 2, c).start()
+        link(1, 0, c).wait_recv()
+        link(1, 2, c).start()
         link(0, 1, c).wait_recv()
         link(0, 2, c).wait_recv()
         for slot in range(n_blk):
@@ -189,7 +191,7 @@
             axis=0,
         ).astype(jnp.bfloat16)
         mixed = jnp.dot(kron[c], x, preferred_element_type=jnp.float32)
-        y = jnp.concatenate(
+        y_ref[...] = jnp.concatenate(
             [
                 jnp.concatenate(
                     [
@@ -204,8 +206,11 @@
             axis=0,
         ).astype(jnp.bfloat16)
 
-        link(1, 0, c).wait_recv()
-        link(1, 2, c).start()
+        @pl.when(c + 1 < cols)
+        def advance():
+            link(0, 0, c + 1).wait_recv()
+            link(0, 2, c + 1).start()
+
         link(1, 1, c).wait_recv()
         link(1, 2, c).wait_recv()
         for half in range(2):
@@ -219,19 +224,23 @@
                 top = r * LANES + half * subs
                 right_pad[top:top + subs, 0:BLOCK] = jnp.where(straight, even, odd)
                 right_pad[top:top + subs, LANES:LANES + BLOCK] = jnp.where(straight, odd, even)
-        result = jnp.dot(y, right_pad[...], preferred_element_type=jnp.float32)
+        result = jnp.dot(y_ref[...], right_pad[...], preferred_element_type=jnp.float32)
         row_live = row96 + row_base < limit_of(out_here, parity)
         for d in range(D):
             rows = slice(d * subs, (d + 1) * subs)
             part = jnp.where(p2[d] == 0, result[rows, 0:BLOCK], result[rows, LANES:LANES + BLOCK])
             live = row_live & (lane96 < limit_of(out_next, (parity + p2[d]) % 2))
-            out_ref[c, :, d * BLOCK:(d + 1) * BLOCK] = jnp.where(live, part, 0.0).astype(jnp.bfloat16)
+            out_own[c, :, d * BLOCK:(d + 1) * BLOCK] = jnp.where(live, part, 0.0).astype(jnp.bfloat16)
+        out_copy(c).start()
         return _
 
+    link(0, 0, 0).wait_recv()
+    link(0, 2, 0).start()
     lax.fori_loop(0, cols, column, 0)
 
     z_copy().wait_send()
     for c in range(cols):
+        out_copy(c).wait()
         for which in range(2):
             for route in range(3):
                 link(which, route, c).wait_send()
@@ -247,7 +256,7 @@
         functools.partial(kernel, cols, subs, n_blk, n_col),
         out_shape=jax.ShapeDtypeStruct(boundary.shape, bf16),
         in_specs=[hbm, hbm, hbm, hbm, smem, smem],
-        out_specs=pl.BlockSpec(memory_space=pltpu.VMEM),
+        out_specs=hbm,
         scratch_shapes=[
             pltpu.VMEM((n_blk, cols, subs, merged), bf16),
             pltpu.VMEM((n_blk, cols, subs, merged), bf16),
@@ -258,10 +267,13 @@
             pltpu.VMEM((cols, KRON, KRON), bf16),
             pltpu.VMEM((2 * LANES, D * LANES), bf16),
             pltpu.VMEM((D * LANES, 2 * LANES), bf16),
+            pltpu.VMEM((D * subs, D * LANES), bf16),
+            pltpu.VMEM(boundary.shape, bf16),
             pltpu.SemaphoreType.DMA((4,)),
             pltpu.SemaphoreType.DMA((2, 3, cols)),
             pltpu.SemaphoreType.DMA((2, 3, cols)),
             pltpu.SemaphoreType.DMA((2,)),
+            pltpu.SemaphoreType.DMA((cols,)),
         ],
         compiler_params=pltpu.CompilerParams(
             collective_id=0, has_side_effects=True

time: 27.5 us -> 23.2 us (0.84)
  Pallas kernels: 25.6 us -> 21.2 us
    pallas_call x1, Pallas kernels: 25.6 us -> 21.2 us  [per_device(): pl.pallas_call(functools.partial(kernel, cols, subs, n_blk, n_col), out_s...]
where the time goes in v3:
time: 23.2 us; the launch traced here: 22.9 us
  Pallas kernels  21.2 us (91%)
  local copies, waits for them, and re-layouts  1.66 us (7%)
    pallas_call x1, Pallas kernels, per_device(): pl.pallas_call(functools.partial(kernel, cols, subs, n_blk, n_col), out_s...  21.2 us
    unnamed x1, local copies, waits for them, and re-layouts  1.66 us

profile of v3, /device:TPU:0, one launch (start us, length us, event | category | flops | bytes accessed | tf_op | source)
XLA Modules:
  0.0 22.9 jit_solution(4858286975755441411)
XLA Ops:
  0.0 21.2 %shard_map.64 = bf16[4,48,576]{2,1,0:T(8,128)(2,1)} custom-call(bf16[4,48,576]{2,1,0:T(8,128)(2,1)} %bound_hbm.1, bf16[864,6]{1,0:T(8,128)(2,1)} %bitcast.5, bf16[4,48,576]{2,1,0:T(8,128)(2,1)} %left_hbm.1, bf16[4,48,576]{2,1,0:T(8,128)(2,1)} %right_hbm.1, s32[3,6,16]{2,1,0:T(8,128)} %bitcast.6, s32[2,16]{1,0:T(2,128)} %bitcast.7), custom_call_target="tpu_custom_call" | custom-call | tf_op jit(solution)/shard_map/pallas_call | solution.py:255
  21.2 1.7 %copy.8 = bf16[4,48,576]{2,1,0:T(8,128)(2,1)} copy(bf16[4,48,576]{2,1,0:T(8,128)(2,1)} %shard_map.64) | data formatting | bytes 442368

commit v4 on v3

--- a/solution.py
+++ b/solution.py
@@ -31,7 +31,7 @@
     cols, subs, n_blk, n_col,
     bound_hbm, row_hbm, left_hbm, right_hbm, legs, charges, out_ref,
     bound_all, right_all, left_own, row_own, row_wide, left_dense, kron, bound_pad, right_pad, y_ref, out_own,
-    local_sem, send_sem, recv_sem, z_sem, out_sem,
+    local_sem, send_sem, recv_sem, z_sem, out_sem, group_in, col_in,
 ):
     me = lax.axis_index("blk")
     here = lax.axis_index("col")
@@ -56,12 +56,29 @@
         copy.start()
 
     barrier = pltpu.get_barrier_semaphore()
-    for target in ({"blk": partner}, {"blk": across}, {"col": col_left}, {"col": col_right}):
-        pl.semaphore_signal(barrier, inc=1, device_id=target, device_id_type=MESH)
+
+    @pl.when(me % 2 == 0)
+    def hub_enters():
+        pl.semaphore_signal(barrier, inc=1, device_id={"blk": across}, device_id_type=MESH)
+
+    @pl.when(me % 2 == 1)
+    def other_enters():
+        pl.semaphore_signal(barrier, inc=1, device_id={"blk": partner}, device_id_type=MESH)
+        pl.semaphore_signal(barrier, inc=1, device_id={"blk": across_partner}, device_id_type=MESH)
+
     bound_pad[...] = jnp.zeros_like(bound_pad)
     right_pad[...] = jnp.zeros_like(right_pad)
     left_dense[...] = jnp.zeros_like(left_dense)
-    pl.semaphore_wait(barrier, 4)
+
+    @pl.when(me % 2 == 0)
+    def hub_knows():
+        pl.semaphore_wait(barrier, n_blk - 1)
+        pl.semaphore_signal(group_in, inc=1, device_id={"blk": partner}, device_id_type=MESH)
+
+    @pl.when(me % 2 == 1)
+    def other_knows():
+        pl.semaphore_wait(group_in, 1)
+        pl.semaphore_signal(barrier, inc=1, device_id={"col": col_right}, device_id_type=MESH)
 
     def z_copy():
         return pltpu.make_async_remote_copy(
@@ -80,7 +97,6 @@
             device_id={"blk": target}, device_id_type=MESH,
         )
 
-    z_copy().start()
     own_copies[0].wait()
     link(0, 0, 0).start()
     own_copies[1].wait()
@@ -95,10 +111,6 @@
             link(1, 1, c).start()
     own_copies[2].wait()
     own_copies[3].wait()
-
-    z_copy().wait_recv()
-    link(1, 0, cols - 1).start()
-    link(1, 1, cols - 1).start()
 
     def scalars(c):
         at = here * cols + c
@@ -157,7 +169,19 @@
         return _
 
     row_wide[:, 0:D] = row_own[...].astype(jnp.float32)
-    lax.fori_loop(0, cols, prepare, 0)
+    lax.fori_loop(0, cols // 2, prepare, 0)
+
+    @pl.when(me % 2 == 1)
+    def other_meets():
+        pl.semaphore_wait(barrier, 1)
+        pl.semaphore_signal(col_in, inc=1, device_id={"blk": partner}, device_id_type=MESH)
+
+    @pl.when(me % 2 == 0)
+    def hub_meets():
+        pl.semaphore_wait(col_in, 1)
+
+    z_copy().start()
+    lax.fori_loop(cols // 2, cols, prepare, 0)
 
     def out_copy(c):
         return pltpu.make_async_copy(out_own.at[c], out_ref.at[c], out_sem.at[c])
@@ -206,6 +230,12 @@
             axis=0,
         ).astype(jnp.bfloat16)
 
+        @pl.when(c == max(cols - 3, 0))
+        def beyond():
+            z_copy().wait_recv()
+            link(1, 0, cols - 1).start()
+            link(1, 1, cols - 1).start()
+
         @pl.when(c + 1 < cols)
         def advance():
             link(0, 0, c + 1).wait_recv()
@@ -274,6 +304,8 @@
             pltpu.SemaphoreType.DMA((2, 3, cols)),
             pltpu.SemaphoreType.DMA((2,)),
             pltpu.SemaphoreType.DMA((cols,)),
+            pltpu.SemaphoreType.REGULAR,
+            pltpu.SemaphoreType.REGULAR,
         ],
         compiler_params=pltpu.CompilerParams(
             collective_id=0, has_side_effects=True

time: 23.2 us -> 20.5 us (0.88)
  Pallas kernels: 21.2 us -> 18.6 us
    pallas_call x1, Pallas kernels: 21.2 us -> 18.6 us  [per_device(): pl.pallas_call(functools.partial(kernel, cols, subs, n_blk, n_col), out_s...]
where the time goes in v4:
time: 20.5 us; the launch traced here: 20.3 us
  Pallas kernels  18.6 us (91%)
  local copies, waits for them, and re-layouts  1.66 us (8%)
    pallas_call x1, Pallas kernels, per_device(): pl.pallas_call(functools.partial(kernel, cols, subs, n_blk, n_col), out_s...  18.6 us
    unnamed x1, local copies, waits for them, and re-layouts  1.66 us

profile of v4, /device:TPU:0, one launch (start us, length us, event | category | flops | bytes accessed | tf_op | source)
XLA Modules:
  0.0 20.3 jit_solution(17945024701398792499)
XLA Ops:
  0.0 18.6 %shard_map.64 = bf16[4,48,576]{2,1,0:T(8,128)(2,1)} custom-call(bf16[4,48,576]{2,1,0:T(8,128)(2,1)} %bound_hbm.1, bf16[864,6]{1,0:T(8,128)(2,1)} %bitcast.5, bf16[4,48,576]{2,1,0:T(8,128)(2,1)} %left_hbm.1, bf16[4,48,576]{2,1,0:T(8,128)(2,1)} %right_hbm.1, s32[3,6,16]{2,1,0:T(8,128)} %bitcast.6, s32[2,16]{1,0:T(2,128)} %bitcast.7), custom_call_target="tpu_custom_call" | custom-call | tf_op jit(solution)/shard_map/pallas_call | solution.py:285
  18.6 1.7 %copy.8 = bf16[4,48,576]{2,1,0:T(8,128)(2,1)} copy(bf16[4,48,576]{2,1,0:T(8,128)(2,1)} %shard_map.64) | data formatting | bytes 442368

commit v5 on v4

--- a/solution.py
+++ b/solution.py
@@ -29,11 +29,13 @@
 
 def kernel(
     cols, subs, n_blk, n_col,
-    bound_hbm, row_hbm, left_hbm, right_hbm, legs, charges, out_ref,
-    bound_all, right_all, left_own, row_own, row_wide, left_dense, kron, bound_pad, right_pad, y_ref, out_own,
-    local_sem, send_sem, recv_sem, z_sem, out_sem, group_in, col_in,
+    bound_hbm, row_hbm, left_hbm, right_hbm, legs_hbm, charges_hbm, out_ref,
+    main_all, tail_all, bound_own, right_own, left_own, row_own, row_wide, left_dense, kron, bound_pad, right_pad, y_ref, out_own,
+    legs, charges, local_sem, send_sem, recv_sem, z_sem, out_sem, group_in, col_in,
 ):
     me = lax.axis_index("blk")
+    wide = D * BLOCK // LANES * LANES
+    rest = D * BLOCK - wide
     here = lax.axis_index("col")
     partner = me + 1 - 2 * (me % 2)
     across = (me + 2) % n_blk
@@ -45,15 +47,24 @@
     row_base = (me % 2) * subs
 
     own_copies = [
-        pltpu.make_async_copy(bound_hbm, bound_all.at[me], local_sem.at[0]),
+        pltpu.make_async_copy(bound_hbm, bound_own, local_sem.at[0]),
         pltpu.make_async_copy(
-            right_hbm.at[pl.ds(1, cols - 1)], right_all.at[me, pl.ds(0, cols - 1)], local_sem.at[1]
+            right_hbm.at[pl.ds(1, cols - 1)], right_own.at[pl.ds(0, cols - 1)], local_sem.at[1]
         ),
         pltpu.make_async_copy(left_hbm, left_own, local_sem.at[2]),
         pltpu.make_async_copy(row_hbm, row_own, local_sem.at[3]),
+        pltpu.make_async_copy(
+            bound_hbm.at[:, :, pl.ds(0, wide)], main_all.at[0, me], local_sem.at[4]
+        ),
+        pltpu.make_async_copy(
+            right_hbm.at[pl.ds(1, cols - 1), :, pl.ds(0, wide)],
+            main_all.at[1, me, pl.ds(0, cols - 1)], local_sem.at[5]
+        ),
+        pltpu.make_async_copy(legs_hbm, legs, local_sem.at[6]),
+        pltpu.make_async_copy(charges_hbm, charges, local_sem.at[7]),
     ]
-    for copy in own_copies:
-        copy.start()
+    for k in (4, 5, 0, 1, 2, 3, 6, 7):
+        own_copies[k].start()
 
     barrier = pltpu.get_barrier_semaphore()
 
@@ -82,35 +93,45 @@
 
     def z_copy():
         return pltpu.make_async_remote_copy(
-            src_ref=right_hbm.at[0], dst_ref=right_all.at[me, cols - 1],
+            src_ref=right_hbm.at[0], dst_ref=right_own.at[cols - 1],
             send_sem=z_sem.at[0], recv_sem=z_sem.at[1],
             device_id={"col": col_left}, device_id_type=MESH,
         )
 
     def link(which, route, c):
-        buffer = bound_all if which == 0 else right_all
         slot = across if route == 2 else me
         target = across if route == 0 else partner
+        piece = tail_all.at[slot, c] if which == 2 else main_all.at[which, slot, c]
         return pltpu.make_async_remote_copy(
-            src_ref=buffer.at[slot, c], dst_ref=buffer.at[slot, c],
+            src_ref=piece, dst_ref=piece,
             send_sem=send_sem.at[which, route, c], recv_sem=recv_sem.at[which, route, c],
             device_id={"blk": target}, device_id_type=MESH,
         )
 
+    own_copies[4].wait()
+    link(0, 0, 0).start()
+    own_copies[5].wait()
+    link(1, 0, 0).start()
+    for c in range(cols):
+        link(0, 1, c).start()
+        if c < cols - 1:
+            link(1, 1, c).start()
     own_copies[0].wait()
-    link(0, 0, 0).start()
     own_copies[1].wait()
+    for c in range(cols - 1):
+        tail_all[me, c] = jnp.concatenate([bound_own[c, :, wide:], right_own[c, :, wide:]], axis=1)
     for c in range(cols):
         if c > 0:
             link(0, 0, c).start()
         if c < cols - 1:
-            link(1, 0, c).start()
-    for c in range(cols):
-        link(0, 1, c).start()
-        if c < cols - 1:
-            link(1, 1, c).start()
+            link(2, 0, c).start()
+            link(2, 1, c).start()
+            if c > 0:
+                link(1, 0, c).start()
     own_copies[2].wait()
     own_copies[3].wait()
+    own_copies[6].wait()
+    own_copies[7].wait()
 
     def scalars(c):
         at = here * cols + c
@@ -183,6 +204,15 @@
     z_copy().start()
     lax.fori_loop(cols // 2, cols, prepare, 0)
 
+    def segment_of(which, slot, c, leg):
+        low = leg * BLOCK
+        if low + BLOCK <= wide:
+            return main_all[which, slot, c, :, low:low + BLOCK]
+        return jnp.concatenate(
+            [main_all[which, slot, c, :, low:wide], tail_all[slot, c, :, which * rest:(which + 1) * rest]],
+            axis=1,
+        )
+
     def out_copy(c):
         return pltpu.make_async_copy(out_own.at[c], out_ref.at[c], out_sem.at[c])
 
@@ -190,14 +220,13 @@
         p0, p1, p2, pr, in_here, out_here, in_next, out_next = scalars(c)
         link(1, 0, c).wait_recv()
         link(1, 2, c).start()
-        link(0, 1, c).wait_recv()
-        link(0, 2, c).wait_recv()
+        for which in (0, 2):
+            link(which, 1, c).wait_recv()
+            link(which, 2, c).wait_recv()
         for slot in range(n_blk):
             top = (slot // 2) * LANES + (slot % 2) * subs
             for u in range(D):
-                bound_pad[top:top + subs, u * LANES:u * LANES + BLOCK] = bound_all[
-                    slot, c, :, u * BLOCK:(u + 1) * BLOCK
-                ]
+                bound_pad[top:top + subs, u * LANES:u * LANES + BLOCK] = segment_of(0, slot, c, u)
         absorbed = jnp.dot(left_dense[c], bound_pad[...], preferred_element_type=jnp.float32)
         high = subs // SUB
         x = jnp.concatenate(
@@ -230,16 +259,22 @@
             axis=0,
         ).astype(jnp.bfloat16)
 
-        @pl.when(c == max(cols - 3, 0))
+        @pl.when(c == 0)
         def beyond():
             z_copy().wait_recv()
-            link(1, 0, cols - 1).start()
-            link(1, 1, cols - 1).start()
+            main_all[1, me, cols - 1] = right_own[cols - 1, :, 0:wide]
+            tail_all[me, cols - 1] = jnp.concatenate(
+                [bound_own[cols - 1, :, wide:], right_own[cols - 1, :, wide:]], axis=1
+            )
+            for route in range(2):
+                link(2, route, cols - 1).start()
+                link(1, route, cols - 1).start()
 
         @pl.when(c + 1 < cols)
         def advance():
-            link(0, 0, c + 1).wait_recv()
-            link(0, 2, c + 1).start()
+            for which in (0, 2):
+                link(which, 0, c + 1).wait_recv()
+                link(which, 2, c + 1).start()
 
         link(1, 1, c).wait_recv()
         link(1, 2, c).wait_recv()
@@ -247,9 +282,8 @@
             even_live = as_mask(row96 + half * subs < in_next).astype(jnp.bfloat16)
             odd_live = as_mask(row96 + half * subs < CHI - in_next).astype(jnp.bfloat16)
             for r in range(D):
-                span = slice(r * BLOCK, (r + 1) * BLOCK)
-                even = right_all[half, c, :, span] * even_live
-                odd = right_all[2 + half, c, :, span] * odd_live
+                even = segment_of(1, half, c, r) * even_live
+                odd = segment_of(1, 2 + half, c, r) * odd_live
                 straight = (parity + pr[r]) % 2 == 0
                 top = r * LANES + half * subs
                 right_pad[top:top + subs, 0:BLOCK] = jnp.where(straight, even, odd)
@@ -264,14 +298,15 @@
         out_copy(c).start()
         return _
 
-    link(0, 0, 0).wait_recv()
-    link(0, 2, 0).start()
+    for which in (0, 2):
+        link(which, 0, 0).wait_recv()
+        link(which, 2, 0).start()
     lax.fori_loop(0, cols, column, 0)
 
     z_copy().wait_send()
     for c in range(cols):
         out_copy(c).wait()
-        for which in range(2):
+        for which in range(3):
             for route in range(3):
                 link(which, route, c).wait_send()
 
@@ -281,15 +316,16 @@
     bf16 = jnp.bfloat16
     row_flat = row_tensor.transpose(1, 2, 3, 0, 4).reshape(D * D * D * cols, D)
     hbm = pl.BlockSpec(memory_space=pl.ANY)
-    smem = pl.BlockSpec(memory_space=pltpu.SMEM)
     return pl.pallas_call(
         functools.partial(kernel, cols, subs, n_blk, n_col),
         out_shape=jax.ShapeDtypeStruct(boundary.shape, bf16),
-        in_specs=[hbm, hbm, hbm, hbm, smem, smem],
+        in_specs=[hbm] * 6,
         out_specs=hbm,
         scratch_shapes=[
-            pltpu.VMEM((n_blk, cols, subs, merged), bf16),
-            pltpu.VMEM((n_blk, cols, subs, merged), bf16),
+            pltpu.VMEM((2, n_blk, cols, subs, merged // LANES * LANES), bf16),
+            pltpu.VMEM((n_blk, cols, subs, LANES), bf16),
+            pltpu.VMEM((cols, subs, merged), bf16),
+            pltpu.VMEM((cols, subs, merged), bf16),
             pltpu.VMEM((cols, subs, merged), bf16),
             pltpu.VMEM(row_flat.shape, bf16),
             pltpu.VMEM((row_flat.shape[0], LANES), jnp.float32),
@@ -299,9 +335,11 @@
             pltpu.VMEM((D * LANES, 2 * LANES), bf16),
             pltpu.VMEM((D * subs, D * LANES), bf16),
             pltpu.VMEM(boundary.shape, bf16),
-            pltpu.SemaphoreType.DMA((4,)),
-            pltpu.SemaphoreType.DMA((2, 3, cols)),
-            pltpu.SemaphoreType.DMA((2, 3, cols)),
+            pltpu.SMEM(leg_parity.shape[1:] + leg_parity.shape[:1], jnp.int32),
+            pltpu.SMEM(bond_charges.shape[::-1], jnp.int32),
+            pltpu.SemaphoreType.DMA((8,)),
+            pltpu.SemaphoreType.DMA((3, 3, cols)),
+            pltpu.SemaphoreType.DMA((3, 3, cols)),
             pltpu.SemaphoreType.DMA((2,)),
             pltpu.SemaphoreType.DMA((cols,)),
             pltpu.SemaphoreType.REGULAR,

time: 20.5 us -> 19.4 us (0.946)
  Pallas kernels: 18.6 us -> 17.6 us
    pallas_call x1, Pallas kernels: 18.6 us -> 17.6 us  [per_device(): pl.pallas_call(functools.partial(kernel, cols, subs, n_blk, n_col), out_s...]
where the time goes in v5:
time: 19.4 us; the launch traced here: 19.3 us
  Pallas kernels  17.6 us (91%)
  local copies, waits for them, and re-layouts  1.66 us (9%)
    pallas_call x1, Pallas kernels, per_device(): pl.pallas_call(functools.partial(kernel, cols, subs, n_blk, n_col), out_s...  17.6 us
    unnamed x1, local copies, waits for them, and re-layouts  1.66 us

profile of v5, /device:TPU:0, one launch (start us, length us, event | category | flops | bytes accessed | tf_op | source)
XLA Modules:
  0.0 19.3 jit_solution(17390995381094743566)
XLA Ops:
  0.0 17.6 %shard_map.64 = bf16[4,48,576]{2,1,0:T(8,128)(2,1)} custom-call(bf16[4,48,576]{2,1,0:T(8,128)(2,1)} %bound_hbm.1, bf16[864,6]{1,0:T(8,128)(2,1)} %bitcast.5, bf16[4,48,576]{2,1,0:T(8,128)(2,1)} %left_hbm.1, bf16[4,48,576]{2,1,0:T(8,128)(2,1)} %right_hbm.1, s32[3,6,16]{2,1,0:T(8,128)} %bitcast.6, s32[2,16]{1,0:T(2,128)} %bitcast.7), custom_call_target="tpu_custom_call" | custom-call | tf_op jit(solution)/shard_map/pallas_call | solution.py:319
  17.6 1.7 %copy.8 = bf16[4,48,576]{2,1,0:T(8,128)(2,1)} copy(bf16[4,48,576]{2,1,0:T(8,128)(2,1)} %shard_map.64) | data formatting | bytes 442368
